TPU v7x, 32 devices: a whole 2x2x4 slice. The times are simulated.
32 devices in a mesh: seq: 8 (over z, x), batch: 4 (over y, core).
Axes of the slice: x: 2, y: 2, z: 4, core: 2. Of those that a mesh axis runs over, the one named last changes fastest.
Arguments:
- hidden: bfloat16 [8, 2048, 4096], P('batch', None, 'seq')
- gain: float32 [4096], P('seq'), may hold values from 0.5 to 1.5
- value_weight: float32 [4096], P('seq'), may hold values from -0.09375 to 0.09375
- rewards: float32 [8, 2048], P('batch', 'seq'), may hold values from -1.5 to 1.5
- reward_mask: int32 [8, 2048], P('batch', 'seq'), may hold values 0 or 1
- lengths: int32 [8], P('batch'), may hold values from 512 to 2048
- horizon: float32 [8], P('batch'), may hold values from 24 to 16384
Outputs:
- advantages: float32 [8, 2048], P(None, ('seq', 'batch'))
- returns: float32 [8, 2048], P(None, ('seq', 'batch'))
All inputs are finite; a program needn't handle non-finite values. No bound on the sum of `reward_mask` on one device may be relied on, other than what follows from the above.
Results may differ from a plain program's by a relative error of at most 0.0003.
Values may be sent and summed in bfloat16 or wider, within the bound.
A program may use at most 64 MiB of HBM per device.

v0:
```python
import jax
import jax.numpy as jnp
from jax import lax
from jax.sharding import PartitionSpec as P

D = 4096


EPS = 1e-05


def from_behind(value, axis, steps):
    count = lax.axis_size(axis)
    initial, last = (max(0, -steps), min(count, count - steps))
    return lax.ppermute(value, axis, [(source, source + steps) for source in range(initial, last)])


def entering(array, axis, combine, identity):
    devices, position = (lax.axis_size(axis), lax.axis_index(axis))
    everything = jax.tree.map(lambda part: lax.all_gather(part, axis), array)
    start = jax.tree.map(
        lambda part, zero: jnp.broadcast_to(jnp.asarray(zero, part.dtype), part.shape),
        array,
        identity,
    )

    def step(k, before):
        at = devices - 1 - k
        reached = at > position
        new = combine(before, jax.tree.map(lambda part: part[at], everything))
        return jax.tree.map(lambda a, b: jnp.where(reached, a, b), new, before)

    return lax.fori_loop(0, devices, step, start)


def per_device(hidden, gain, value_weight, rewards, reward_mask, lengths, horizon):
    my_index = lax.axis_index("seq")
    block = rewards.shape[1]
    wide_rows = hidden.astype(jnp.float32)
    part_squares = jnp.sum(wide_rows * wide_rows, -1)
    part_projected = jnp.sum(wide_rows * (gain * value_weight), -1)
    squares, projected = (
        lax.psum_scatter(part_squares, "seq", scatter_dimension=1, tiled=True),
        lax.psum_scatter(part_projected, "seq", scatter_dimension=1, tiled=True),
    )
    values = projected * lax.rsqrt(squares / D + EPS)
    positions = my_index * block + jnp.arange(block, dtype=jnp.int32)
    valid = (positions[None, :] < lengths[:, None]).astype(jnp.float32)
    next_valid = (positions[None, :] + 1 < lengths[:, None]).astype(jnp.float32)
    following = from_behind(values[:, 0], "seq", -1)
    next_values = jnp.concatenate([values[:, 1:], following[:, None]], 1)
    delta = (rewards * reward_mask.astype(jnp.float32) + next_valid * next_values - values) * valid
    log_decay = -1.0 / horizon
    offsets = jnp.arange(block, dtype=jnp.int32)
    distance = (offsets[None, :] - offsets[:, None]).astype(jnp.float32)
    upper_mask = distance >= 0.0
    powers = jnp.where(
        upper_mask[None], jnp.exp(jnp.maximum(distance, 0.0)[None] * log_decay[:, None, None]), 0.0
    )
    local_gae = jnp.einsum("rtk,rk->rt", powers, delta, precision=lax.Precision.HIGHEST)
    tail_decay = jnp.exp((block - offsets).astype(jnp.float32)[None, :] * log_decay[:, None])
    start_value = local_gae[:, 0]
    block_decay = jnp.exp(block * log_decay)

    def compose(earlier, later):
        return (later[0] + later[1] * earlier[0], later[1] * earlier[1])

    carry_in, _ = entering(
        (start_value, block_decay),
        "seq",
        compose,
        (jnp.zeros_like(start_value), jnp.ones_like(block_decay)),
    )
    gae = local_gae + tail_decay * carry_in[:, None]
    returns = (gae + values) * valid
    count, first, second = lax.psum(
        (jnp.sum(valid), jnp.sum(gae), jnp.sum(gae * gae)), ("seq", "batch")
    )
    mean = first / count
    var = jnp.maximum(second / count - mean * mean, 1.0)
    whitened = (gae - mean) * valid * lax.rsqrt(var)
    out_adv, out_returns = (
        lax.all_to_all(whitened, "batch", split_axis=1, concat_axis=0, tiled=True),
        lax.all_to_all(returns, "batch", split_axis=1, concat_axis=0, tiled=True),
    )
    return (out_adv, out_returns)


def solution(mesh):
    return jax.shard_map(
        per_device,
        mesh=mesh,
        in_specs=(
            P("batch", None, "seq"),
            P("seq"),
            P("seq"),
            P("batch", "seq"),
            P("batch", "seq"),
            P("batch"),
            P("batch"),
        ),
        out_specs=(P(None, ("seq", "batch")), P(None, ("seq", "batch"))),
        check_vma=False,
    )
```

profile of v0, /device:TPU:0, one launch (start us, length us, event | category | flops | bytes accessed | tf_op | source)
XLA Modules:
  0.0 239.1 jit_solution(13834046668706539538)
XLA Ops:
  7.2 0.7 mul.99
  7.9 3.7 %fusion.2 = (f32[2,2048]{1,0:T(2,128)S(1)}, f32[2,2048]{1,0:T(2,128)S(1)}) fusion(bf16[2,2048,512]{2,1,0:T(8,128)(2,1)} %param.9, f32[512]{0:T(512)S(1)} %mul.99), kind=kLoop, calls=%fused_computation.7 | loop fusion | flops 10477568 | bytes 4229120 | tf_op jit(solution)/shard_map/reduce_sum | solution.py:40
  11.7 1.4 copy.23
  13.1 1.4 copy.25
  14.7 0.6 dynamic-slice
  16.0 0.1 exponential_dynamic-update-slice_fusion
  16.1 64.5 %reduce-scatter.7.cloned.1.call-done = f32[256,2]{1,0:T(8,128)} async-done(((f32[2048,2]{1,0:T(8,128)}), f32[256,2]{1,0:T(8,128)}) %reduce-scatter.7.cloned.1.call-update) | async-done | bytes 2064
  80.6 1.0 copy.24
  81.5 65.6 %reduce-scatter.9.cloned.1.call-done = f32[256,2]{1,0:T(8,128)} async-done(((f32[2048,2]{1,0:T(8,128)}), f32[256,2]{1,0:T(8,128)}) %reduce-scatter.9.cloned.1.call-update) | async-done | bytes 2064
  147.1 1.0 copy.26
  148.1 0.1 slice_reduce_fusion.1
  148.3 1.3 collective-permute-start
  149.6 4.2 %collective-permute-done = f32[2]{0:T(128)S(1)} collective-permute-done((f32[2]{0:T(128)S(1)}, f32[2]{0:T(128)S(1)}, u32[]{:S(2)}, u32[]{:S(2)}) %collective-permute-start) | collective-permute-done | bytes 40 | tf_op jit(solution)/shard_map/ppermute | solution.py:15
  153.9 0.7 fusion.3
  154.6 0.1 slice_reduce_fusion
  154.8 0.2 dynamic-update-slice
  155.0 19.1 %all-reduce.3 = (f32[16]{0:T(128)S(1)}, f32[16]{0:T(128)S(1)}) all-reduce(f32[16]{0:T(128)S(1)} %dynamic-update-slice, f32[16]{0:T(128)S(1)} %get-tuple-element.174), channel_id=2, replica_groups=mesh['seq'=8,'batch'=4] {'seq'}, use_global_device_ids=true, to_apply=%add | all-reduce | flops 32 | bytes 256
  174.2 0.4 while.16
  174.6 0.7 compare_select_fusion
  175.3 0.7 fusion.18
  176.0 37.1 %all-reduce.2 = (f32[]{:T(128)}, f32[]{:T(128)}, f32[]{:T(128)}) all-reduce(f32[]{:T(128)} %get-tuple-element.156, f32[]{:T(128)} %get-tuple-element.176, f32[]{:T(128)} %get-tuple-element.155), channel_id=1, replica_groups=mesh['seq'=8,'batch'=4] {'seq','batch'}, use_global_device_ids=true, to_apply=%region_11.12 | all-reduce | flops 3 | bytes 24 | tf_op jit(solution)/shard_map/psum | solution.py:76
  215.9 0.7 reshape.73
  216.5 3.7 %all-to-all-start = ((f32[4,1,128]{2,1,0:T(1,128)}), f32[4,1,128]{2,1,0:T(1,128)S(1)}, u32[]{:S(2)}, u32[]{:S(2)}) async-start(f32[4,1,128]{2,1,0:T(1,128)} %reshape.73), calls=%async_computation | async-start | bytes 4096 | tf_op jit(solution)/shard_map/all_to_all | solution.py:83
  220.3 0.7 reshape.75
  221.0 2.9 %all-to-all-done = f32[4,1,128]{2,1,0:T(1,128)S(1)} async-done(((f32[4,1,128]{2,1,0:T(1,128)}), f32[4,1,128]{2,1,0:T(1,128)S(1)}, u32[]{:S(2)}, u32[]{:S(2)}) %all-to-all-start) | async-done | bytes 2080 | tf_op jit(solution)/shard_map/all_to_all | solution.py:83
  224.0 3.2 %all-to-all-start.1 = ((f32[4,1,128]{2,1,0:T(1,128)}), f32[4,1,128]{2,1,0:T(1,128)S(1)}, u32[]{:S(2)}, u32[]{:S(2)}) async-start(f32[4,1,128]{2,1,0:T(1,128)} %reshape.75), calls=%async_computation.1 | async-start | bytes 4096 | tf_op jit(solution)/shard_map/all_to_all | solution.py:84
  227.2 0.5 broadcast.83
  227.7 0.7 reduce.4
  228.4 0.7 reshape.74
  229.1 1.9 all-to-all-done.1
  231.0 0.7 reduce.5
  231.6 0.7 reshape.76
  (41 shorter events, 1.1 us)
Async XLA Ops:
  7.2 73.4 %reduce-scatter.7.cloned.1.call-start = ((), (), s32[]{:S(2)}) async-start(), calls=%async_computation.4 | async-start | bytes 1179648
  7.9 6.8 %copy-start.4 = (u32[32]{0:T(128)S(1)}, u32[32]{0:T(128)}, u32[]{:S(2)}) copy-start(u32[32]{0:T(128)} %constant.81) | copy-start | bytes 388
  7.9 8.0 %copy-start.3 = (f32[2]{0:T(128)S(1)}, f32[2]{0:T(128)}, u32[]{:S(2)}) copy-start(f32[2]{0:T(128)} %param.15) | copy-start | bytes 28
  7.9 145.9 %copy-start = (s32[2]{0:T(128)S(1)}, s32[2]{0:T(128)}, u32[]{:S(2)}) copy-start(s32[2]{0:T(128)} %param.14) | copy-start | bytes 28
  7.9 145.9 %copy-start.1 = (f32[2,256]{1,0:T(2,128)S(1)}, f32[2,256]{1,0:T(2,128)}, u32[]{:S(2)}) copy-start(f32[2,256]{1,0:T(2,128)} %param.12) | copy-start | bytes 6148
  7.9 145.9 %copy-start.2 = (s32[2,256]{1,0:T(2,128)S(1)}, s32[2,256]{1,0:T(2,128)}, u32[]{:S(2)}) copy-start(s32[2,256]{1,0:T(2,128)} %param.13) | copy-start | bytes 6148
  13.1 134.0 %reduce-scatter.9.cloned.1.call-start = ((), (), s32[]{:S(2)}) async-start(), calls=%async_computation.5 | async-start | bytes 1179648
  148.3 5.5 %collective-permute-start = (f32[2]{0:T(128)S(1)}, f32[2]{0:T(128)S(1)}, u32[]{:S(2)}, u32[]{:S(2)}) collective-permute-start(f32[2]{0:T(128)S(1)} %slice_reduce_fusion.1), channel_id=1, source_target_pairs={{4,0},{8,4},{12,8},{16,12},{20,16},{24,20},{28,24},{5,1},{9,5},{13... | collective-permute-start | bytes 32 | tf_op jit(solution)/shard_map/ppermute | solution.py:15
  216.5 7.4 %all-to-all-start = ((f32[4,1,128]{2,1,0:T(1,128)}), f32[4,1,128]{2,1,0:T(1,128)S(1)}, u32[]{:S(2)}, u32[]{:S(2)}) async-start(f32[4,1,128]{2,1,0:T(1,128)} %reshape.73), calls=%async_computation | async-start | bytes 4096 | tf_op jit(solution)/shard_map/all_to_all | solution.py:83
  224.0 7.0 %all-to-all-start.1 = ((f32[4,1,128]{2,1,0:T(1,128)}), f32[4,1,128]{2,1,0:T(1,128)S(1)}, u32[]{:S(2)}, u32[]{:S(2)}) async-start(f32[4,1,128]{2,1,0:T(1,128)} %reshape.75), calls=%async_computation.1 | async-start | bytes 4096 | tf_op jit(solution)/shard_map/all_to_all | solution.py:84
Sparse Core Ops, SparseCore 0:
  13.2 67.3 reduce-scatter.6
  84.0 63.0 reduce-scatter.8
where the time goes:
time: 240 us; the launch traced here: 239 us
  waiting for transfers between devices  139 us (58%)
  blocking collectives  56.2 us (23%)
  between operations  17.5 us (7%)
  local copies, waits for them, and re-layouts  9.54 us (4%)
  starting transfers between devices  8.35 us (3%)
  other arithmetic  7.63 us (3%)
    unnamed x4, waiting for transfers between devices  130 us
    psum x1, blocking collectives, per_device(): lax.psum((jnp.sum(valid), jnp.sum(gae), jnp.sum(gae * gae)), ('seq', 'bat...  37.1 us
    unnamed x1, blocking collectives  19.1 us
    unnamed x22, local copies, waits for them, and re-layouts  8.28 us
  transfers between devices with their start and end apart: 5, of which 5 were waited for; matrix products, arithmetic and copies ran while one was open for 2% of the time, Pallas kernels for 0%

commit v1 on v0

v1 whole, which is shorter than its diff:
```python
import functools

import jax
import jax.numpy as jnp
from jax import lax
from jax.experimental import pallas as pl
from jax.experimental.pallas import tpu as pltpu
from jax.sharding import PartitionSpec as P

EPS = 1e-05
LANES = 128
F32 = jnp.float32


def kernel(n, nb, owners, hidden, gain, weight, rewards, mask, lengths, horizon,
           adv_ref, ret_ref,
           hv, gain_v, weight_v, rew_v, mask_v, len_s, hor_s,
           part, rbuf, rw_send, rw_recv, len_send, len_recv, hor_send, hor_recv,
           sum_send, sum_recv, tok_send, tok_recv,
           chunk_sem, small_sem, part_ss, part_rs, rw_ss, rw_rs, info_ss, info_rs,
           sum_ss, sum_rs, tok_ss, tok_rs):
    R, T, depth = hidden.shape
    block = rewards.shape[1]
    width = block // nb
    per = n // owners
    base = (n - owners) // 2
    L = T // owners
    G = L // LANES
    gb = block // LANES
    rows = G * R
    total = depth * n
    everyone = n * nb
    s = lax.axis_index("seq")
    b = lax.axis_index("batch")
    is_owner = (s >= base) & (s < base + owners)
    mine = s - base
    out_o = s // per
    rw_at = base + out_o
    half = s % per

    def chunk_copy(o):
        span = pl.ds(o * L, L)
        return pltpu.make_async_copy(hidden.at[:, span, :], hv.at[:, span, :], chunk_sem.at[o])

    smalls = [
        pltpu.make_async_copy(src, dst, small_sem.at[i])
        for i, (src, dst) in enumerate(
            ((gain, gain_v), (weight, weight_v), (rewards, rew_v), (mask, mask_v),
             (lengths, len_s), (horizon, hor_s)))
    ]
    for copy in smalls:
        copy.start()
    for o in range(owners):
        chunk_copy(o).start()
    barrier = pltpu.get_barrier_semaphore()
    for k in range(1, n):
        pl.semaphore_signal(barrier, inc=1, device_id={"seq": (s + k) % n},
                            device_id_type=pl.DeviceIdType.MESH)
    for k in range(1, nb):
        pl.semaphore_signal(barrier, inc=1, device_id={"batch": (b + k) % nb},
                            device_id_type=pl.DeviceIdType.MESH)
    for copy in smalls:
        copy.wait()

    head = (gain_v[...] * weight_v[...]).reshape(1, depth)
    high = head.astype(jnp.bfloat16).astype(F32)
    middle = (head - high).astype(jnp.bfloat16).astype(F32)
    low = head - high - middle
    wrow = lax.broadcasted_iota(jnp.int32, (16, depth), 0)
    pieces = jnp.where(wrow == 0, high, jnp.where(wrow == 1, middle, jnp.where(wrow == 2, low, 0.0)))
    pieces = pieces.astype(jnp.bfloat16)

    rw = rew_v[...] * mask_v[...].astype(F32)
    for g in range(gb):
        rw_send[g * R:(g + 1) * R, :] = rw[:, g * LANES:(g + 1) * LANES]
    for r in range(R):
        len_send[r:r + 1, :] = jnp.full((1, LANES), len_s[r], jnp.int32)
        hor_send[r:r + 1, :] = jnp.full((1, LANES), hor_s[r], F32)

    diagonal = (lax.broadcasted_iota(jnp.int32, (LANES, LANES), 0)
                == lax.broadcasted_iota(jnp.int32, (LANES, LANES), 1))

    def compute(o, carry):
        chunk_copy(o).wait()
        for g in range(G):
            for r in range(R):
                at = pl.ds(pl.multiple_of(o * L + g * LANES, LANES), LANES)
                h = hv[r, at, :]
                both = lax.dot_general(jnp.concatenate([h, pieces], 0), h,
                                       (((1,), (1,)), ((), ())), preferred_element_type=F32)
                row = g * R + r
                part[o, 0, row:row + 1, :] = jnp.sum(both[LANES:LANES + 8], 0, keepdims=True)
                part[o, 1, row:row + 1, :] = jnp.sum(
                    jnp.where(diagonal, both[:LANES], 0.0), 0, keepdims=True)
        return carry

    lax.fori_loop(0, owners, compute, 0)

    pl.semaphore_wait(barrier, n - 1 + nb - 1)

    def part_copy(o):
        return pltpu.make_async_remote_copy(
            part.at[o], rbuf.at[s], part_ss.at[o], part_rs.at[s],
            device_id={"seq": base + o}, device_id_type=pl.DeviceIdType.MESH)

    def rw_copy():
        return pltpu.make_async_remote_copy(
            rw_send, rw_recv.at[half], rw_ss, rw_rs.at[half],
            device_id={"seq": rw_at}, device_id_type=pl.DeviceIdType.MESH)

    for o in range(owners):
        @pl.when(base + o != s)
        def _():
            part_copy(o).start()

    @pl.when(rw_at != s)
    def _():
        rw_copy().start()

    @pl.when(rw_at == s)
    def _():
        rw_recv[half] = rw_send[...]

    infos = []
    for k in range(1, nb):
        for i, (src, dst) in enumerate(((len_send, len_recv), (hor_send, hor_recv))):
            infos.append((k, i, src, dst))

    def info_copy(k, i, src, dst):
        return pltpu.make_async_remote_copy(
            src, dst.at[b], info_ss.at[i, k], info_rs.at[i, b],
            device_id={"batch": (b + k) % nb}, device_id_type=pl.DeviceIdType.MESH)

    def info_arrived(k, i, src, dst):
        at = (b + k) % nb
        return pltpu.make_async_remote_copy(
            src, dst.at[at], info_ss.at[i, k], info_rs.at[i, at],
            device_id={"batch": at}, device_id_type=pl.DeviceIdType.MESH)

    for entry in infos:
        info_copy(*entry).start()
    len_recv[b] = len_send[...]
    hor_recv[b] = hor_send[...]

    def sum_copy(k):
        to = (s * nb + b + k) % everyone
        return pltpu.make_async_remote_copy(
            sum_send, sum_recv.at[mine, b], sum_ss.at[k], sum_rs.at[mine, b],
            device_id={"seq": to // nb, "batch": to % nb}, device_id_type=pl.DeviceIdType.MESH)

    def tok_copy(h, c):
        g = h * gb + (c * width) // LANES
        return pltpu.make_async_remote_copy(
            tok_send.at[g], tok_recv.at[b], tok_ss.at[h, c], tok_rs.at[b],
            device_id={"seq": mine * per + h, "batch": c}, device_id_type=pl.DeviceIdType.MESH)

    @pl.when(is_owner)
    def _():
        row = lax.broadcasted_iota(jnp.int32, (rows, LANES), 0)
        lane = lax.broadcasted_iota(jnp.int32, (rows, LANES), 1)
        group = row // R
        which = row % R
        length = jnp.full((rows, LANES), len_s[0], jnp.int32)
        reach = jnp.full((rows, LANES), hor_s[0], F32)
        for r in range(1, R):
            length = jnp.where(which == r, len_s[r], length)
            reach = jnp.where(which == r, hor_s[r], reach)
        rate = -1.0 / reach
        local = group * LANES + lane
        token = mine * L + local
        valid = (token < length).astype(F32)
        next_valid = (token + 1 < length).astype(F32)
        steps = [1 << i for i in range(LANES.bit_length() - 1)]
        lane_decay = [jnp.where(lane < LANES - k, jnp.exp(rate * k), 0.0) for k in steps]
        hops = [1 << i for i in range(max(G - 1, 0).bit_length())]
        row_decay = [jnp.where(group + k < G, jnp.exp(rate * (k * LANES)), 0.0) for k in hops]
        into = jnp.where(group < G - 1, jnp.exp(rate * (LANES - lane).astype(F32)), 0.0)
        power = jnp.exp(rate * (L - 1 - local).astype(F32))
        decay = jnp.exp(rate)
        power_sum = jnp.sum(power, 1, keepdims=True)
        power_squares = jnp.sum(power * power, 1, keepdims=True)

        for h in range(per):
            @pl.when(mine * per + h != s)
            def _():
                pltpu.make_async_remote_copy(
                    rw_send, rw_recv.at[h], rw_ss, rw_rs.at[h],
                    device_id={"seq": s}, device_id_type=pl.DeviceIdType.MESH).wait_recv()
        gains = jnp.concatenate([rw_recv[h] for h in range(per)], 0)

        rbuf[s] = part[mine]
        for k in range(1, n):
            at = (s + k) % n
            pltpu.make_async_remote_copy(
                part.at[0], rbuf.at[at], part_ss.at[0], part_rs.at[at],
                device_id={"seq": at}, device_id_type=pl.DeviceIdType.MESH).wait_recv()
        projected = rbuf[0, 0]
        squares = rbuf[0, 1]
        for k in range(1, n):
            projected = projected + rbuf[k, 0]
            squares = squares + rbuf[k, 1]
        values = projected * lax.rsqrt(squares / total + EPS)
        ahead = pltpu.roll(values, LANES - 1, 1)
        if G > 1:
            after = jnp.where(group < G - 1, pltpu.roll(ahead, rows - R, 0), 0.0)
        else:
            after = jnp.zeros_like(ahead)
        next_values = jnp.where(lane == LANES - 1, after, ahead)
        gae = (gains + next_valid * next_values - values) * valid
        for k, factor in zip(steps, lane_decay):
            gae = gae + factor * pltpu.roll(gae, LANES - k, 1)
        if G > 1:
            start = jnp.broadcast_to(gae[:, 0:1], (rows, LANES))
            for k, factor in zip(hops, row_decay):
                start = start + factor * pltpu.roll(start, rows - k * R, 0)
            gae = gae + into * pltpu.roll(start, rows - R, 0)
        for g in range(G):
            tok_send[g, 0] = gae[g * R:(g + 1) * R]
            tok_send[g, 1] = values[g * R:(g + 1) * R]
        for h in range(per):
            for c in range(nb):
                self_copy = (mine * per + h == s) & (b == c)

                @pl.when(jnp.logical_not(self_copy))
                def _():
                    tok_copy(h, c).start()

                @pl.when(self_copy)
                def _():
                    tok_recv[b] = tok_send[h * gb + (c * width) // LANES]
        sums = jnp.where(lane == 1, jnp.sum(gae, 1, keepdims=True), 0.0)
        sums = jnp.where(lane == 2, 2.0 * jnp.sum(gae * power, 1, keepdims=True), sums)
        sums = jnp.where(lane == 3, jnp.sum(gae * gae, 1, keepdims=True), sums)
        sums = jnp.where(lane == 4, power_sum, sums)
        sums = jnp.where(lane == 5, power_squares, sums)
        sums = jnp.where((lane == 0) & (group == 0), values + decay * gae, sums)
        summary = sums[0:R]
        for g in range(1, G):
            summary = summary + sums[g * R:(g + 1) * R]
        sum_send[...] = summary
        sum_recv[mine, b] = summary
        if everyone <= 32:
            for k in range(1, everyone):
                sum_copy(k).start()
        else:
            def start(k, carry):
                sum_copy(k).start()
                return carry
            lax.fori_loop(1, everyone, start, 0)

    for entry in infos:
        info_arrived(*entry).wait_recv()
    lane = lax.broadcasted_iota(jnp.int32, (R, LANES), 1)
    group_out = half * gb + (b * width) // LANES
    local = group_out * LANES + lane
    token = out_o * L + local
    count = jnp.zeros((R, LANES), F32)
    jump, power_out, valid_out, lens = [], [], [], []
    for c in range(nb):
        length = len_recv[c]
        rate = -1.0 / hor_recv[c]
        count = count + jnp.minimum(length, T).astype(F32)
        jump.append(jnp.exp(rate * float(L)))
        power_out.append(jnp.exp(rate * (L - 1 - local).astype(F32)))
        valid_out.append((token < length).astype(F32))
        lens.append(length)
    count = jnp.sum(count, 0, keepdims=True)

    for o in range(owners):
        for c in range(nb):
            @pl.when((base + o != s) | (b != c))
            def _():
                pltpu.make_async_remote_copy(
                    sum_send, sum_recv.at[o, c], sum_ss.at[0], sum_rs.at[o, c],
                    device_id={"seq": base + o, "batch": c},
                    device_id_type=pl.DeviceIdType.MESH).wait_recv()

    acc = jnp.zeros((R, LANES), F32)
    entering = []
    for c in range(nb):
        u = jnp.zeros((R, LANES), F32)
        chosen = jnp.zeros((R, LANES), F32)
        for o in reversed(range(owners)):
            message = sum_recv[o, c]
            factor = jnp.where((lane == 1) | (lane == 3), 1.0,
                               jnp.where((lane == 2) | (lane == 4), u,
                                         jnp.where(lane == 5, u * u, 0.0)))
            acc = acc + message * factor
            chosen = jnp.where(out_o == o, u, chosen)
            if o:
                first_value = jnp.broadcast_to(message[:, 0:1], (R, LANES))
                u = jnp.where(o * L < lens[c], first_value + jump[c] * u, 0.0)
        entering.append(chosen)
    acc = jnp.sum(acc, 0, keepdims=True)
    lane1 = lax.broadcasted_iota(jnp.int32, (1, LANES), 1)
    first = jnp.sum(jnp.where((lane1 == 1) | (lane1 == 4), acc, 0.0), 1, keepdims=True)
    second = jnp.sum(jnp.where((lane1 == 2) | (lane1 == 3) | (lane1 == 5), acc, 0.0), 1, keepdims=True)
    mean = first / count
    var = jnp.maximum(second / count - mean * mean, 1.0)
    scale = lax.rsqrt(var)

    for c in range(nb):
        @pl.when((rw_at != s) | (b != c))
        def _():
            pltpu.make_async_remote_copy(
                tok_send.at[0], tok_recv.at[c], tok_ss.at[0, 0], tok_rs.at[c],
                device_id={"seq": rw_at, "batch": c},
                device_id_type=pl.DeviceIdType.MESH).wait_recv()
    spots = LANES // width
    spot = b % spots

    def pick(x):
        result = x[:, 0:width]
        for j in range(1, spots):
            result = jnp.where(spot == j, x[:, j * width:(j + 1) * width], result)
        return result

    for c in range(nb):
        gae = tok_recv[c, 0] + power_out[c] * entering[c]
        ret_ref[c * R:(c + 1) * R, :] = pick((gae + tok_recv[c, 1]) * valid_out[c])
        adv_ref[c * R:(c + 1) * R, :] = pick((gae - mean) * valid_out[c] * scale)

    for o in range(owners):
        @pl.when(base + o != s)
        def _():
            part_copy(o).wait_send()

    @pl.when(rw_at != s)
    def _():
        rw_copy().wait_send()

    for entry in infos:
        info_copy(*entry).wait_send()

    @pl.when(is_owner)
    def _():
        for h in range(per):
            for c in range(nb):
                @pl.when((mine * per + h != s) | (b != c))
                def _():
                    tok_copy(h, c).wait_send()
        if everyone <= 32:
            for k in range(1, everyone):
                sum_copy(k).wait_send()
        else:
            def finish(k, carry):
                sum_copy(k).wait_send()
                return carry
            lax.fori_loop(1, everyone, finish, 0)


def per_device(hidden, gain, weight, rewards, mask, lengths, horizon):
    n = lax.axis_size("seq")
    nb = lax.axis_size("batch")
    owners = n // 2 if n % 4 == 0 else n
    R, T, depth = hidden.shape
    block = rewards.shape[1]
    per = n // owners
    G = T // owners // LANES
    gb = block // LANES
    rows = G * R
    everyone = n * nb
    dma = pltpu.SemaphoreType.DMA
    out = jax.ShapeDtypeStruct((R * nb, block // nb), F32)
    return pl.pallas_call(
        functools.partial(kernel, n, nb, owners),
        out_shape=(out, out),
        in_specs=[pl.BlockSpec(memory_space=pl.ANY)] * 7,
        out_specs=(pl.BlockSpec(memory_space=pltpu.VMEM),) * 2,
        scratch_shapes=[
            pltpu.VMEM((R, T, depth), jnp.bfloat16),
            pltpu.VMEM((depth,), F32),
            pltpu.VMEM((depth,), F32),
            pltpu.VMEM((R, block), F32),
            pltpu.VMEM((R, block), jnp.int32),
            pltpu.SMEM((R,), jnp.int32),
            pltpu.SMEM((R,), F32),
            pltpu.VMEM((owners, 2, rows, LANES), F32),
            pltpu.VMEM((n, 2, rows, LANES), F32),
            pltpu.VMEM((gb * R, LANES), F32),
            pltpu.VMEM((per, gb * R, LANES), F32),
            pltpu.VMEM((R, LANES), jnp.int32),
            pltpu.VMEM((nb, R, LANES), jnp.int32),
            pltpu.VMEM((R, LANES), F32),
            pltpu.VMEM((nb, R, LANES), F32),
            pltpu.VMEM((R, LANES), F32),
            pltpu.VMEM((owners, nb, R, LANES), F32),
            pltpu.VMEM((G, 2, R, LANES), F32),
            pltpu.VMEM((nb, 2, R, LANES), F32),
            dma((owners,)), dma((6,)),
            dma((owners,)), dma((n,)),
            dma(()), dma((per,)),
            dma((2, nb)), dma((2, nb)),
            dma((everyone,)), dma((owners, nb)),
            dma((per, nb)), dma((nb,)),
        ],
        compiler_params=pltpu.CompilerParams(collective_id=0, has_side_effects=True),
    )(hidden, gain, weight, rewards, mask, lengths, horizon)


def solution(mesh):
    return jax.shard_map(
        per_device,
        mesh=mesh,
        in_specs=(
            P("batch", None, "seq"),
            P("seq"),
            P("seq"),
            P("batch", "seq"),
            P("batch", "seq"),
            P("batch"),
            P("batch"),
        ),
        out_specs=(P(None, ("seq", "batch")), P(None, ("seq", "batch"))),
        check_vma=False,
    )
```

time: 240 us -> 20.4 us (0.08)
  waiting for transfers between devices: 139 us -> 0 us
  blocking collectives: 56.2 us -> 0 us
  Pallas kernels: 0 us -> 17 us
  between operations: 17.5 us -> 0.64 us
  starting transfers between devices: 8.35 us -> 0 us
  other arithmetic: 7.63 us -> 0 us
  local copies, waits for them, and re-layouts: 9.54 us -> 2.53 us
    unnamed x4 -> x0, waiting for transfers between devices: 130 us -> none
    psum x1 -> x0, blocking collectives: 37.1 us -> none  [per_device(): lax.psum((jnp.sum(valid), jnp.sum(gae), jnp.sum(gae * gae)), ('seq', 'bat...]
    unnamed x1 -> x0, blocking collectives: 19.1 us -> none
    pallas_call x0 -> x1, Pallas kernels: none -> 17 us  [per_device(): pl.pallas_call(functools.partial(kernel, n, nb, owners), out_shape=(out,...]
    all_to_all x2 -> x0, starting transfers between devices: 6.97 us -> none  [the longest x1 3.73 us: per_device(): lax.all_to_all(whitened, 'batch', split_axis=1, concat_axis=0, tiled=True)]
    unnamed x22 -> x2, local copies, waits for them, and re-layouts: 8.28 us -> 2.53 us
    all_to_all x2 -> x0, waiting for transfers between devices: 4.83 us -> none  [the longest x1 2.94 us: per_device(): lax.all_to_all(whitened, 'batch', split_axis=1, concat_axis=0, tiled=True)]
    reduce_sum x2 -> x0, other arithmetic: 4.42 us -> none  [the longest x1 3.73 us: per_device(): part_squares = jnp.sum(wide_rows * wide_rows, -1)]
  transfers between devices with their start and end apart: 5 -> 0, of which waited for: 5 -> 0; matrix products, arithmetic and copies ran while one was open for 2% -> 0% of each run, Pallas kernels for 0% -> 0%
where the time goes in v1:
time: 20.4 us; the launch traced here: 20.2 us
  Pallas kernels  17 us (83%)
  local copies, waits for them, and re-layouts  2.53 us (12%)
  between operations  0.64 us (3%)
    pallas_call x1, Pallas kernels, per_device(): pl.pallas_call(functools.partial(kernel, n, nb, owners), out_shape=(out,...  17 us
    unnamed x2, local copies, waits for them, and re-layouts  2.53 us

profile of v1, /device:TPU:0, one launch (start us, length us, event | category | flops | bytes accessed | tf_op | source)
XLA Modules:
  0.0 20.2 jit_solution(206986969740311196)
XLA Ops:
  0.6 17.0 %shard_map.86 = (f32[8,64]{1,0:T(8,128)}, f32[8,64]{1,0:T(8,128)}) custom-call(bf16[2,2048,512]{2,1,0:T(8,128)(2,1)} %hidden.1, f32[512]{0:T(512)} %gain.1, f32[512]{0:T(512)} %weight.1, f32[2,256]{1,0:T(2,128)} %rewards.1, s32[2,256]{1,0:T(2,128)} %mask.1, s32[2]{0:T(128)} %lengths.1, f32[2]{0:T(128)} %horizon.1), custom_call_target="tpu_custom_call" | custom-call | tf_op jit(solution)/shard_map/pallas_call | solution.py:365
  17.6 1.3 %copy.11 = f32[8,64]{1,0:T(8,128)} copy(f32[8,64]{1,0:T(8,128)} %get-tuple-element.4) | data formatting | bytes 4096
  18.9 1.3 %copy.12 = f32[8,64]{1,0:T(8,128)} copy(f32[8,64]{1,0:T(8,128)} %get-tuple-element.5) | data formatting | bytes 4096

commit v2 on v1

--- a/solution.py
+++ b/solution.py
@@ -13,7 +13,7 @@
 
 
 def kernel(n, nb, owners, hidden, gain, weight, rewards, mask, lengths, horizon,
-           adv_ref, ret_ref,
+           out_ref,
            hv, gain_v, weight_v, rew_v, mask_v, len_s, hor_s,
            part, rbuf, rw_send, rw_recv, len_send, len_recv, hor_send, hor_recv,
            sum_send, sum_recv, tok_send, tok_recv,
@@ -50,12 +50,25 @@
     ]
     for copy in smalls:
         copy.start()
-    for o in range(owners):
-        chunk_copy(o).start()
+    near_high = s * (owners // 2) // n
+    near_low = s % 2
+
+    def turn(k):
+        back = owners - 1 - k
+        if owners % 2:
+            return (s + back) % owners
+        return (near_high + back // 2) % (owners // 2) * 2 + (near_low + back) % 2
+
+    for k in range(owners):
+        chunk_copy(turn(k)).start()
     barrier = pltpu.get_barrier_semaphore()
     for k in range(1, n):
-        pl.semaphore_signal(barrier, inc=1, device_id={"seq": (s + k) % n},
-                            device_id_type=pl.DeviceIdType.MESH)
+        peer = (s + k) % n
+
+        @pl.when(is_owner | ((peer >= base) & (peer < base + owners)))
+        def _():
+            pl.semaphore_signal(barrier, inc=1, device_id={"seq": peer},
+                                device_id_type=pl.DeviceIdType.MESH)
     for k in range(1, nb):
         pl.semaphore_signal(barrier, inc=1, device_id={"batch": (b + k) % nb},
                             device_id_type=pl.DeviceIdType.MESH)
@@ -80,7 +93,41 @@
     diagonal = (lax.broadcasted_iota(jnp.int32, (LANES, LANES), 0)
                 == lax.broadcasted_iota(jnp.int32, (LANES, LANES), 1))
 
-    def compute(o, carry):
+    infos = []
+    for k in range(1, nb):
+        for i, (src, dst) in enumerate(((len_send, len_recv), (hor_send, hor_recv))):
+            infos.append((k, i, src, dst))
+
+    def info_copy(k, i, src, dst):
+        return pltpu.make_async_remote_copy(
+            src, dst.at[b], info_ss.at[i, k], info_rs.at[i, b],
+            device_id={"batch": (b + k) % nb}, device_id_type=pl.DeviceIdType.MESH)
+
+    def info_arrived(k, i, src, dst):
+        at = (b + k) % nb
+        return pltpu.make_async_remote_copy(
+            src, dst.at[at], info_ss.at[i, k], info_rs.at[i, at],
+            device_id={"batch": at}, device_id_type=pl.DeviceIdType.MESH)
+
+    def part_copy(o):
+        return pltpu.make_async_remote_copy(
+            part.at[o], rbuf.at[s], part_ss.at[o], part_rs.at[s],
+            device_id={"seq": base + o}, device_id_type=pl.DeviceIdType.MESH)
+
+    def rw_copy():
+        return pltpu.make_async_remote_copy(
+            rw_send, rw_recv.at[half], rw_ss, rw_rs.at[half],
+            device_id={"seq": rw_at}, device_id_type=pl.DeviceIdType.MESH)
+
+    def send_part(o):
+        @pl.when(base + o != s)
+        def _():
+            part_copy(o).start()
+
+    meet = min(1, owners - 1)
+
+    def compute(k, carry):
+        o = turn(k)
         chunk_copy(o).wait()
         for g in range(G):
             for r in range(R):
@@ -92,53 +139,32 @@
                 part[o, 0, row:row + 1, :] = jnp.sum(both[LANES:LANES + 8], 0, keepdims=True)
                 part[o, 1, row:row + 1, :] = jnp.sum(
                     jnp.where(diagonal, both[:LANES], 0.0), 0, keepdims=True)
+
+        @pl.when(k == meet)
+        def _():
+            met = jnp.where(is_owner, n - 1, owners) + nb - 1
+            pl.semaphore_wait(barrier, met)
+            for before in range(meet):
+                send_part(turn(before))
+
+            @pl.when(rw_at != s)
+            def _():
+                rw_copy().start()
+
+            for entry in infos:
+                info_copy(*entry).start()
+
+        @pl.when(k >= meet)
+        def _():
+            send_part(o)
         return carry
 
     lax.fori_loop(0, owners, compute, 0)
-
-    pl.semaphore_wait(barrier, n - 1 + nb - 1)
-
-    def part_copy(o):
-        return pltpu.make_async_remote_copy(
-            part.at[o], rbuf.at[s], part_ss.at[o], part_rs.at[s],
-            device_id={"seq": base + o}, device_id_type=pl.DeviceIdType.MESH)
-
-    def rw_copy():
-        return pltpu.make_async_remote_copy(
-            rw_send, rw_recv.at[half], rw_ss, rw_rs.at[half],
-            device_id={"seq": rw_at}, device_id_type=pl.DeviceIdType.MESH)
-
-    for o in range(owners):
-        @pl.when(base + o != s)
-        def _():
-            part_copy(o).start()
-
-    @pl.when(rw_at != s)
-    def _():
-        rw_copy().start()
 
     @pl.when(rw_at == s)
     def _():
         rw_recv[half] = rw_send[...]
 
-    infos = []
-    for k in range(1, nb):
-        for i, (src, dst) in enumerate(((len_send, len_recv), (hor_send, hor_recv))):
-            infos.append((k, i, src, dst))
-
-    def info_copy(k, i, src, dst):
-        return pltpu.make_async_remote_copy(
-            src, dst.at[b], info_ss.at[i, k], info_rs.at[i, b],
-            device_id={"batch": (b + k) % nb}, device_id_type=pl.DeviceIdType.MESH)
-
-    def info_arrived(k, i, src, dst):
-        at = (b + k) % nb
-        return pltpu.make_async_remote_copy(
-            src, dst.at[at], info_ss.at[i, k], info_rs.at[i, at],
-            device_id={"batch": at}, device_id_type=pl.DeviceIdType.MESH)
-
-    for entry in infos:
-        info_copy(*entry).start()
     len_recv[b] = len_send[...]
     hor_recv[b] = hor_send[...]
 
@@ -317,8 +343,8 @@
 
     for c in range(nb):
         gae = tok_recv[c, 0] + power_out[c] * entering[c]
-        ret_ref[c * R:(c + 1) * R, :] = pick((gae + tok_recv[c, 1]) * valid_out[c])
-        adv_ref[c * R:(c + 1) * R, :] = pick((gae - mean) * valid_out[c] * scale)
+        out_ref[(nb + c) * R:(nb + c + 1) * R, :] = pick((gae + tok_recv[c, 1]) * valid_out[c])
+        out_ref[c * R:(c + 1) * R, :] = pick((gae - mean) * valid_out[c] * scale)
 
     for o in range(owners):
         @pl.when(base + o != s)
@@ -361,12 +387,11 @@
     rows = G * R
     everyone = n * nb
     dma = pltpu.SemaphoreType.DMA
-    out = jax.ShapeDtypeStruct((R * nb, block // nb), F32)
-    return pl.pallas_call(
+    both = pl.pallas_call(
         functools.partial(kernel, n, nb, owners),
-        out_shape=(out, out),
+        out_shape=pltpu.VMEM((2 * R * nb, block // nb), F32),
         in_specs=[pl.BlockSpec(memory_space=pl.ANY)] * 7,
-        out_specs=(pl.BlockSpec(memory_space=pltpu.VMEM),) * 2,
+        out_specs=pl.BlockSpec(memory_space=pltpu.VMEM),
         scratch_shapes=[
             pltpu.VMEM((R, T, depth), jnp.bfloat16),
             pltpu.VMEM((depth,), F32),
@@ -396,6 +421,7 @@
         ],
         compiler_params=pltpu.CompilerParams(collective_id=0, has_side_effects=True),
     )(hidden, gain, weight, rewards, mask, lengths, horizon)
+    return both[:R * nb], both[R * nb:]
 
 
 def solution(mesh):

time: 20.4 us -> 17.6 us (0.86)
  local copies, waits for them, and re-layouts: 2.53 us -> 0.6 us
  Pallas kernels: 17 us -> 16.2 us
    unnamed x2 -> x0, local copies, waits for them, and re-layouts: 2.53 us -> none
    pallas_call x1, Pallas kernels: 17 us -> 16.2 us  [per_device(): pl.pallas_call(functools.partial(kernel, n, nb, owners), out_shape=pltpu....]
    slice x0 -> x1, local copies, waits for them, and re-layouts: none -> 0.6 us  [per_device(): return (both[:R * nb], both[R * nb:])]
where the time goes in v2:
time: 17.6 us; the launch traced here: 17.4 us
  Pallas kernels  16.2 us (92%)
  between operations  0.64 us (4%)
  local copies, waits for them, and re-layouts  0.6 us (3%)
    pallas_call x1, Pallas kernels, per_device(): pl.pallas_call(functools.partial(kernel, n, nb, owners), out_shape=pltpu....  16.2 us
    slice x1, local copies, waits for them, and re-layouts, per_device(): return (both[:R * nb], both[R * nb:])  0.6 us

profile of v2, /device:TPU:0, one launch (start us, length us, event | category | flops | bytes accessed | tf_op | source)
XLA Modules:
  0.0 17.4 jit_solution(8302516430296375575)
XLA Ops:
  0.6 16.2 %shard_map.86 = f32[16,64]{1,0:T(8,128)S(1)} custom-call(bf16[2,2048,512]{2,1,0:T(8,128)(2,1)} %hidden.1, f32[512]{0:T(512)} %gain.1, f32[512]{0:T(512)} %weight.1, f32[2,256]{1,0:T(2,128)} %rewards.1, s32[2,256]{1,0:T(2,128)} %mask.1, s32[2]{0:T(128)} %lengths.1, f32[2]{0:T(128)} %horizon.1), custom_call_target="tpu_custom_call" | custom-call | tf_op jit(solution)/shard_map/pallas_call | solution.py:390
  16.8 0.6 %fusion = (f32[8,64]{1,0:T(8,128)}, f32[8,64]{1,0:T(8,128)}) fusion(f32[16,64]{1,0:T(8,128)S(1)} %shard_map.86), kind=kLoop, calls=%fused_computation | loop fusion | bytes 8192 | tf_op jit(solution)/shard_map/slice | solution.py:424

commit v3 on v2

--- a/solution.py
+++ b/solution.py
@@ -29,7 +29,6 @@
     gb = block // LANES
     rows = G * R
     total = depth * n
-    everyone = n * nb
     s = lax.axis_index("seq")
     b = lax.axis_index("batch")
     is_owner = (s >= base) & (s < base + owners)
@@ -38,9 +37,9 @@
     rw_at = base + out_o
     half = s % per
 
-    def chunk_copy(o):
+    def chunk_copy(o, r):
         span = pl.ds(o * L, L)
-        return pltpu.make_async_copy(hidden.at[:, span, :], hv.at[:, span, :], chunk_sem.at[o])
+        return pltpu.make_async_copy(hidden.at[r, span, :], hv.at[r, span, :], chunk_sem.at[o, r])
 
     smalls = [
         pltpu.make_async_copy(src, dst, small_sem.at[i])
@@ -60,7 +59,8 @@
         return (near_high + back // 2) % (owners // 2) * 2 + (near_low + back) % 2
 
     for k in range(owners):
-        chunk_copy(turn(k)).start()
+        for r in range(R):
+            chunk_copy(turn(k), r).start()
     barrier = pltpu.get_barrier_semaphore()
     for k in range(1, n):
         peer = (s + k) % n
@@ -70,7 +70,7 @@
             pl.semaphore_signal(barrier, inc=1, device_id={"seq": peer},
                                 device_id_type=pl.DeviceIdType.MESH)
     for k in range(1, nb):
-        pl.semaphore_signal(barrier, inc=1, device_id={"batch": (b + k) % nb},
+        pl.semaphore_signal(barrier, inc=1, device_id={"batch": lax.rem(b + k, nb)},
                             device_id_type=pl.DeviceIdType.MESH)
     for copy in smalls:
         copy.wait()
@@ -90,9 +90,6 @@
         len_send[r:r + 1, :] = jnp.full((1, LANES), len_s[r], jnp.int32)
         hor_send[r:r + 1, :] = jnp.full((1, LANES), hor_s[r], F32)
 
-    diagonal = (lax.broadcasted_iota(jnp.int32, (LANES, LANES), 0)
-                == lax.broadcasted_iota(jnp.int32, (LANES, LANES), 1))
-
     infos = []
     for k in range(1, nb):
         for i, (src, dst) in enumerate(((len_send, len_recv), (hor_send, hor_recv))):
@@ -101,10 +98,10 @@
     def info_copy(k, i, src, dst):
         return pltpu.make_async_remote_copy(
             src, dst.at[b], info_ss.at[i, k], info_rs.at[i, b],
-            device_id={"batch": (b + k) % nb}, device_id_type=pl.DeviceIdType.MESH)
+            device_id={"batch": lax.rem(b + k, nb)}, device_id_type=pl.DeviceIdType.MESH)
 
     def info_arrived(k, i, src, dst):
-        at = (b + k) % nb
+        at = lax.rem(b + k, nb)
         return pltpu.make_async_remote_copy(
             src, dst.at[at], info_ss.at[i, k], info_rs.at[i, at],
             device_id={"batch": at}, device_id_type=pl.DeviceIdType.MESH)
@@ -128,17 +125,20 @@
 
     def compute(k, carry):
         o = turn(k)
-        chunk_copy(o).wait()
-        for g in range(G):
-            for r in range(R):
+        for r in range(R):
+            chunk_copy(o, r).wait()
+            for g in range(G):
                 at = pl.ds(pl.multiple_of(o * L + g * LANES, LANES), LANES)
                 h = hv[r, at, :]
-                both = lax.dot_general(jnp.concatenate([h, pieces], 0), h,
-                                       (((1,), (1,)), ((), ())), preferred_element_type=F32)
+                sums = lax.dot_general(pieces, h, (((1,), (1,)), ((), ())),
+                                       preferred_element_type=F32)
+                squares = jnp.zeros((LANES, LANES), F32)
+                for j in range(depth // LANES):
+                    wide = h[:, j * LANES:(j + 1) * LANES].astype(F32)
+                    squares = squares + wide * wide
                 row = g * R + r
-                part[o, 0, row:row + 1, :] = jnp.sum(both[LANES:LANES + 8], 0, keepdims=True)
-                part[o, 1, row:row + 1, :] = jnp.sum(
-                    jnp.where(diagonal, both[:LANES], 0.0), 0, keepdims=True)
+                part[o, 0, row:row + 1, :] = jnp.sum(sums[0:8], 0, keepdims=True)
+                part[o, 1, row:row + 1, :] = jnp.sum(squares.T, 0, keepdims=True)
 
         @pl.when(k == meet)
         def _():
@@ -168,17 +168,40 @@
     len_recv[b] = len_send[...]
     hor_recv[b] = hor_send[...]
 
-    def sum_copy(k):
-        to = (s * nb + b + k) % everyone
-        return pltpu.make_async_remote_copy(
-            sum_send, sum_recv.at[mine, b], sum_ss.at[k], sum_rs.at[mine, b],
-            device_id={"seq": to // nb, "batch": to % nb}, device_id_type=pl.DeviceIdType.MESH)
-
-    def tok_copy(h, c):
+    def sum_copy(i, j):
+        return pltpu.make_async_remote_copy(
+            sum_send, sum_recv.at[mine, b], sum_ss.at[i, j], sum_rs.at[mine, b],
+            device_id={"seq": i, "batch": j}, device_id_type=pl.DeviceIdType.MESH)
+
+    def each_sum(act):
+        def one(i):
+            for j in range(nb):
+                if isinstance(i, int) and not base <= i < base + owners:
+                    act(sum_copy(i, j))
+                else:
+                    @pl.when((i != s) | (j != b))
+                    def _():
+                        act(sum_copy(i, j))
+
+        if n * nb <= 32:
+            for i in range(n):
+                one(i)
+        else:
+            def body(i, carry):
+                one(i)
+                return carry
+            lax.fori_loop(0, n, body, 0)
+
+    def tok_copy(h, j):
+        c = lax.rem(b + j, nb)
         g = h * gb + (c * width) // LANES
         return pltpu.make_async_remote_copy(
-            tok_send.at[g], tok_recv.at[b], tok_ss.at[h, c], tok_rs.at[b],
+            tok_send.at[g], tok_recv.at[b], tok_ss.at[h, j], tok_rs.at[b],
             device_id={"seq": mine * per + h, "batch": c}, device_id_type=pl.DeviceIdType.MESH)
+
+    def tok_local(h):
+        g = h * gb + (b * width) // LANES
+        return pltpu.make_async_copy(tok_send.at[g], tok_recv.at[b], tok_rs.at[b])
 
     @pl.when(is_owner)
     def _():
@@ -196,8 +219,9 @@
         token = mine * L + local
         valid = (token < length).astype(F32)
         next_valid = (token + 1 < length).astype(F32)
-        steps = [1 << i for i in range(LANES.bit_length() - 1)]
-        lane_decay = [jnp.where(lane < LANES - k, jnp.exp(rate * k), 0.0) for k in steps]
+        levels = [[j * k for j in range(1, min(8, LANES // k))] for k in (1, 8, 64)]
+        lane_decay = [[jnp.where(lane < LANES - k, jnp.exp(rate * k), 0.0) for k in level]
+                      for level in levels]
         hops = [1 << i for i in range(max(G - 1, 0).bit_length())]
         row_decay = [jnp.where(group + k < G, jnp.exp(rate * (k * LANES)), 0.0) for k in hops]
         into = jnp.where(group < G - 1, jnp.exp(rate * (LANES - lane).astype(F32)), 0.0)
@@ -233,8 +257,9 @@
             after = jnp.zeros_like(ahead)
         next_values = jnp.where(lane == LANES - 1, after, ahead)
         gae = (gains + next_valid * next_values - values) * valid
-        for k, factor in zip(steps, lane_decay):
-            gae = gae + factor * pltpu.roll(gae, LANES - k, 1)
+        for level, factors in zip(levels, lane_decay):
+            terms = [factor * pltpu.roll(gae, LANES - k, 1) for k, factor in zip(level, factors)]
+            gae = gae + sum(terms[1:], terms[0])
         if G > 1:
             start = jnp.broadcast_to(gae[:, 0:1], (rows, LANES))
             for k, factor in zip(hops, row_decay):
@@ -243,17 +268,6 @@
         for g in range(G):
             tok_send[g, 0] = gae[g * R:(g + 1) * R]
             tok_send[g, 1] = values[g * R:(g + 1) * R]
-        for h in range(per):
-            for c in range(nb):
-                self_copy = (mine * per + h == s) & (b == c)
-
-                @pl.when(jnp.logical_not(self_copy))
-                def _():
-                    tok_copy(h, c).start()
-
-                @pl.when(self_copy)
-                def _():
-                    tok_recv[b] = tok_send[h * gb + (c * width) // LANES]
         sums = jnp.where(lane == 1, jnp.sum(gae, 1, keepdims=True), 0.0)
         sums = jnp.where(lane == 2, 2.0 * jnp.sum(gae * power, 1, keepdims=True), sums)
         sums = jnp.where(lane == 3, jnp.sum(gae * gae, 1, keepdims=True), sums)
@@ -264,15 +278,31 @@
         for g in range(1, G):
             summary = summary + sums[g * R:(g + 1) * R]
         sum_send[...] = summary
-        sum_recv[mine, b] = summary
-        if everyone <= 32:
-            for k in range(1, everyone):
-                sum_copy(k).start()
-        else:
-            def start(k, carry):
-                sum_copy(k).start()
-                return carry
-            lax.fori_loop(1, everyone, start, 0)
+        pltpu.make_async_copy(sum_send, sum_recv.at[mine, b], sum_rs.at[mine, b]).start()
+        each_sum(lambda copy: copy.start())
+        for h in range(per):
+            for j in range(1, nb):
+                tok_copy(h, j).start()
+
+            @pl.when(mine * per + h == s)
+            def _():
+                tok_local(h).start()
+
+            @pl.when(mine * per + h != s)
+            def _():
+                tok_copy(h, 0).start()
+
+    for o in range(owners):
+        @pl.when(base + o != s)
+        def _():
+            part_copy(o).wait_send()
+
+    @pl.when(rw_at != s)
+    def _():
+        rw_copy().wait_send()
+
+    for entry in infos:
+        info_copy(*entry).wait_send()
 
     for entry in infos:
         info_arrived(*entry).wait_recv()
@@ -292,14 +322,23 @@
         lens.append(length)
     count = jnp.sum(count, 0, keepdims=True)
 
+    @pl.when(is_owner)
+    def _():
+        each_sum(lambda copy: copy.wait_send())
+        for h in range(per):
+            for j in range(1, nb):
+                tok_copy(h, j).wait_send()
+
+            @pl.when(mine * per + h != s)
+            def _():
+                tok_copy(h, 0).wait_send()
+
     for o in range(owners):
         for c in range(nb):
-            @pl.when((base + o != s) | (b != c))
-            def _():
-                pltpu.make_async_remote_copy(
-                    sum_send, sum_recv.at[o, c], sum_ss.at[0], sum_rs.at[o, c],
-                    device_id={"seq": base + o, "batch": c},
-                    device_id_type=pl.DeviceIdType.MESH).wait_recv()
+            pltpu.make_async_remote_copy(
+                sum_send, sum_recv.at[o, c], sum_ss.at[0, 0], sum_rs.at[o, c],
+                device_id={"seq": base + o, "batch": c},
+                device_id_type=pl.DeviceIdType.MESH).wait_recv()
 
     acc = jnp.zeros((R, LANES), F32)
     entering = []
@@ -326,12 +365,10 @@
     scale = lax.rsqrt(var)
 
     for c in range(nb):
-        @pl.when((rw_at != s) | (b != c))
-        def _():
-            pltpu.make_async_remote_copy(
-                tok_send.at[0], tok_recv.at[c], tok_ss.at[0, 0], tok_rs.at[c],
-                device_id={"seq": rw_at, "batch": c},
-                device_id_type=pl.DeviceIdType.MESH).wait_recv()
+        pltpu.make_async_remote_copy(
+            tok_send.at[0], tok_recv.at[c], tok_ss.at[0, 0], tok_rs.at[c],
+            device_id={"seq": rw_at, "batch": c},
+            device_id_type=pl.DeviceIdType.MESH).wait_recv()
     spots = LANES // width
     spot = b % spots
 
@@ -345,34 +382,6 @@
         gae = tok_recv[c, 0] + power_out[c] * entering[c]
         out_ref[(nb + c) * R:(nb + c + 1) * R, :] = pick((gae + tok_recv[c, 1]) * valid_out[c])
         out_ref[c * R:(c + 1) * R, :] = pick((gae - mean) * valid_out[c] * scale)
-
-    for o in range(owners):
-        @pl.when(base + o != s)
-        def _():
-            part_copy(o).wait_send()
-
-    @pl.when(rw_at != s)
-    def _():
-        rw_copy().wait_send()
-
-    for entry in infos:
-        info_copy(*entry).wait_send()
-
-    @pl.when(is_owner)
-    def _():
-        for h in range(per):
-            for c in range(nb):
-                @pl.when((mine * per + h != s) | (b != c))
-                def _():
-                    tok_copy(h, c).wait_send()
-        if everyone <= 32:
-            for k in range(1, everyone):
-                sum_copy(k).wait_send()
-        else:
-            def finish(k, carry):
-                sum_copy(k).wait_send()
-                return carry
-            lax.fori_loop(1, everyone, finish, 0)
 
 
 def per_device(hidden, gain, weight, rewards, mask, lengths, horizon):
@@ -385,7 +394,6 @@
     G = T // owners // LANES
     gb = block // LANES
     rows = G * R
-    everyone = n * nb
     dma = pltpu.SemaphoreType.DMA
     both = pl.pallas_call(
         functools.partial(kernel, n, nb, owners),
@@ -412,11 +420,11 @@
             pltpu.VMEM((owners, nb, R, LANES), F32),
             pltpu.VMEM((G, 2, R, LANES), F32),
             pltpu.VMEM((nb, 2, R, LANES), F32),
-            dma((owners,)), dma((6,)),
+            dma((owners, R)), dma((6,)),
             dma((owners,)), dma((n,)),
             dma(()), dma((per,)),
             dma((2, nb)), dma((2, nb)),
-            dma((everyone,)), dma((owners, nb)),
+            dma((n, nb)), dma((owners, nb)),
             dma((per, nb)), dma((nb,)),
         ],
         compiler_params=pltpu.CompilerParams(collective_id=0, has_side_effects=True),

time: 17.6 us -> 17.5 us (level)
  no operation moved by 1% of the time
where the time goes in v3:
time: 17.5 us; the launch traced here: 17.3 us
  Pallas kernels  16.1 us (92%)
  between operations  0.64 us (4%)
  local copies, waits for them, and re-layouts  0.6 us (3%)
    pallas_call x1, Pallas kernels, per_device(): pl.pallas_call(functools.partial(kernel, n, nb, owners), out_shape=pltpu....  16.1 us
    slice x1, local copies, waits for them, and re-layouts, per_device(): return (both[:R * nb], both[R * nb:])  0.6 us

profile of v3, /device:TPU:0, one launch (start us, length us, event | category | flops | bytes accessed | tf_op | source)
XLA Modules:
  0.0 17.3 jit_solution(512348994866865005)
XLA Ops:
  0.6 16.1 %shard_map.86 = f32[16,64]{1,0:T(8,128)S(1)} custom-call(bf16[2,2048,512]{2,1,0:T(8,128)(2,1)} %hidden.1, f32[512]{0:T(512)} %gain.1, f32[512]{0:T(512)} %weight.1, f32[2,256]{1,0:T(2,128)} %rewards.1, s32[2,256]{1,0:T(2,128)} %mask.1, s32[2]{0:T(128)} %lengths.1, f32[2]{0:T(128)} %horizon.1), custom_call_target="tpu_custom_call" | custom-call | tf_op jit(solution)/shard_map/pallas_call | solution.py:398
  16.7 0.6 %fusion = (f32[8,64]{1,0:T(8,128)}, f32[8,64]{1,0:T(8,128)}) fusion(f32[16,64]{1,0:T(8,128)S(1)} %shard_map.86), kind=kLoop, calls=%fused_computation | loop fusion | bytes 8192 | tf_op jit(solution)/shard_map/slice | solution.py:432
